TPU v7x, 1024 devices: a whole 8x8x8 slice. The times are simulated.
1024 devices in a mesh: dp: 8 (over z_lo, core), ctx: 8 (over y), head: 16 (over x, z_hi).
Axes of the slice: x: 8, y: 8, z: 8 (z_hi: 2, z_lo: 4; z = z_hi * 4 + z_lo), core: 2. Of those that a mesh axis runs over, the one named last changes fastest.
Arguments:
- latent: bfloat16 [8, 1024, 512], P('dp', 'ctx'), may hold values from -6 to 6
- rope: bfloat16 [8, 1024, 64], P('dp', 'ctx'), may hold values from -6 to 6
- query: bfloat16 [8, 1024, 12288], P('dp', 'ctx', 'head'), may hold values from -9 to 9
- grad_out: bfloat16 [8, 1024, 8192], P('dp', 'ctx', 'head'), may hold values from -6 to 6
- attn_out: bfloat16 [8, 1024, 8192], P('dp', 'ctx', 'head'), may hold values from -40 to 40
- lse: float32 [8, 64, 1024], P('dp', 'head', 'ctx'), may hold values from -100 to 100, as said below
- positions: int32 [8, 1024], P('dp'), may hold values from 0 to 1023, as said below
- w_uk: bfloat16 [512, 8192], P(None, 'head'), may hold values from -2 to 2
- w_uv: bfloat16 [512, 8192], P(None, 'head'), may hold values from -2 to 2
Outputs:
- grad_query: bfloat16 [8, 1024, 12288], P('dp', 'ctx', 'head')
- grad_latent: float32 [8, 1024, 512], P('dp', 'ctx')
- grad_rope: float32 [8, 1024, 64], P('dp', 'ctx')
- grad_wuk: bfloat16 [512, 8192], P(('dp', 'ctx'), 'head')
- grad_wuv: bfloat16 [512, 8192], P(('dp', 'ctx'), 'head')
Inputs may be any that keep to these rules, and one draw needn't show every extreme that they name: Each sequence's row is a permutation of 0 to 1023 made of runs of 64 consecutive positions, each run filling an aligned run of 64 rows in rising order; which run goes to which rows is drawn. lse[h, i] is the log of the sum of exp(scores[i, j]) over the keys j with positions[j] <= positions[i].
All inputs are finite; a program needn't handle non-finite values.
Results may differ from a plain program's by a relative error of at most 0.02.
Values may be sent and summed in bfloat16 or wider, within the bound.
A program may use at most 64 MiB of HBM per device.

v0:
```python
import math

import jax
import jax.numpy as jnp
from jax import lax
from jax.sharding import PartitionSpec as P

DR = 64
DN = 128
DV = 128


MASKED = -1e30


def in_one_piece(arrays, axis, dim, along):
    both = jnp.concatenate(arrays, axis=along)
    result, at, finished = (lax.all_gather(both, axis, axis=dim, tiled=True), 0, [])
    for a in arrays:
        finished.append(lax.slice_in_dim(result, at, at + a.shape[along], axis=along))
        at += a.shape[along]
    return tuple(finished)


def split_up(shard, dim, peers):
    before, after = (shard.shape[:dim], shard.shape[dim + 1 :])
    return jnp.moveaxis(shard.reshape(*before, peers, -1, *after), dim, 0)


def sent_and_summed(shard, axis, dim):
    peers = lax.axis_size(axis)
    parts = lax.all_to_all(split_up(shard, dim, peers), axis, 0, 0, tiled=True)
    return jnp.sum(parts.astype(jnp.float32), axis=0)


def together(arrays, axis):
    line, at, finished = (jnp.concatenate([a.reshape(-1) for a in arrays]), 0, [])
    so_far = lax.psum(line, axis)
    for a in arrays:
        finished.append(so_far[at : at + a.size].reshape(a.shape))
        at += a.size
    return tuple(finished)


def sent_together(arrays, axis, dim, along):
    both = jnp.concatenate(arrays, axis=along)
    result, at, finished = (sent_and_summed(both, axis, dim), 0, [])
    for a in arrays:
        finished.append(lax.slice_in_dim(result, at, at + a.shape[along], axis=along))
        at += a.shape[along]
    return tuple(finished)


def block_grads(
    queries, grads, lse_rows, delta_rows, query_pos, key_rows, value_rows, key_pos, score_scale
):
    scores = (
        jnp.einsum("grd,gsd->grs", queries, key_rows, preferred_element_type=jnp.float32)
        * score_scale
    )
    allowed = key_pos[None, None, :] <= query_pos[None, :, None]
    weights = jnp.exp(jnp.where(allowed, scores - lse_rows[:, :, None], MASKED))
    dots = jnp.einsum("grd,gsd->grs", grads, value_rows, preferred_element_type=jnp.float32)
    score_grad = (weights * (dots - delta_rows[:, :, None]) * score_scale).astype(jnp.bfloat16)
    weights_b = weights.astype(jnp.bfloat16)
    return (score_grad, weights_b)


def head_grads(
    queries, grads, lse_rows, delta_rows, query_pos, key_rows, value_rows, key_pos, score_scale
):
    score_grad, weights_b = block_grads(
        queries, grads, lse_rows, delta_rows, query_pos, key_rows, value_rows, key_pos, score_scale
    )
    query_grad = jnp.einsum(
        "grs,gsd->grd", score_grad, key_rows, preferred_element_type=jnp.float32
    )
    key_grad = jnp.einsum("grs,grd->gsd", score_grad, queries, preferred_element_type=jnp.float32)
    value_grad = jnp.einsum("grs,grd->gsd", weights_b, grads, preferred_element_type=jnp.float32)
    return (query_grad, key_grad, value_grad)


def guarded_grads(
    queries, grads, lse_rows, delta_rows, query_pos, key_rows, value_rows, key_pos, score_scale
):

    def skipped():
        return (
            jnp.zeros(queries.shape, jnp.float32),
            jnp.zeros(key_rows.shape, jnp.float32),
            jnp.zeros(value_rows.shape, jnp.float32),
        )

    def computed():
        return head_grads(
            queries,
            grads,
            lse_rows,
            delta_rows,
            query_pos,
            key_rows,
            value_rows,
            key_pos,
            score_scale,
        )

    return lax.cond(jnp.min(key_pos) > jnp.max(query_pos), skipped, computed)


def head_major(flat, row_count, head_count, width):
    return flat.reshape(row_count, head_count, width).transpose(1, 0, 2)


def row_major(stacked):
    return stacked.transpose(1, 0, 2).reshape(stacked.shape[1], stacked.shape[0] * stacked.shape[2])


def on_device(latent, rope, query, grad_out, attn_out, lse, positions, w_uk, w_uv):
    latent_rows = latent[0]
    row_count = latent_rows.shape[0]
    head_count = w_uk.shape[1] // DN
    score_scale = 1.0 / math.sqrt(DN + DR)
    highest = lax.Precision.HIGHEST
    my_index = lax.axis_index("ctx")
    seq_order = positions[0]
    key_pos = lax.dynamic_slice_in_dim(seq_order, my_index * row_count, row_count)
    queries = head_major(query[0], row_count, head_count, DN + DR)
    grads = head_major(grad_out[0], row_count, head_count, DV)
    outputs = head_major(attn_out[0], row_count, head_count, DV)
    delta_rows = jnp.sum(grads.astype(jnp.float32) * outputs.astype(jnp.float32), axis=2)
    lse_rows = lse[0]
    nope_keys = head_major(
        jnp.dot(latent_rows, w_uk, preferred_element_type=jnp.float32).astype(jnp.bfloat16),
        row_count,
        head_count,
        DN,
    )
    value_rows = head_major(
        jnp.dot(latent_rows, w_uv, preferred_element_type=jnp.float32).astype(jnp.bfloat16),
        row_count,
        head_count,
        DV,
    )
    rope_keys = jnp.broadcast_to(rope[0][None, :, :], (head_count, row_count, DR))
    key_rows = jnp.concatenate([nope_keys, rope_keys], axis=2)
    lse_all, delta_all = in_one_piece((lse_rows, delta_rows), "ctx", 1, 0)
    piece_query, piece_grads = in_one_piece((queries, grads), "ctx", 1, 2)
    query_grad, key_grad, value_grad = guarded_grads(
        piece_query,
        piece_grads,
        lse_all,
        delta_all,
        seq_order,
        key_rows,
        value_rows,
        key_pos,
        score_scale,
    )
    query_all = query_grad
    query_all, key_total, value_total = (query_all, key_grad, value_grad)
    query_total = sent_and_summed(query_all.astype(jnp.bfloat16), "ctx", 1)
    key_nope = row_major(key_total[:, :, :DN])
    value_flat = row_major(value_total)
    rope_part = jnp.sum(key_total[:, :, DN:], axis=0)
    latent_part = jnp.dot(key_nope, w_uk.astype(jnp.float32).T, precision=highest) + jnp.dot(
        value_flat, w_uv.astype(jnp.float32).T, precision=highest
    )
    latent_f = latent_rows.astype(jnp.float32).T
    weight_uk = jnp.dot(latent_f, key_nope, precision=highest)
    weight_uv = jnp.dot(latent_f, value_flat, precision=highest)
    latent_grad, rope_grad = tuple(
        (
            part.astype(jnp.float32)
            for part in together(
                (latent_part.astype(jnp.bfloat16), rope_part.astype(jnp.bfloat16)), "head"
            )
        )
    )
    weight_uk, weight_uv = sent_together(
        (weight_uk.astype(jnp.bfloat16), weight_uv.astype(jnp.bfloat16)), ("dp", "ctx"), 0, 1
    )
    query_out = row_major(query_total).astype(jnp.bfloat16)
    return (
        query_out[None],
        latent_grad[None],
        rope_grad[None],
        weight_uk.astype(jnp.bfloat16),
        weight_uv.astype(jnp.bfloat16),
    )


def solution(mesh):
    return jax.shard_map(
        on_device,
        mesh=mesh,
        in_specs=(
            P("dp", "ctx", None),
            P("dp", "ctx", None),
            P("dp", "ctx", "head"),
            P("dp", "ctx", "head"),
            P("dp", "ctx", "head"),
            P("dp", "head", "ctx"),
            P("dp", None),
            P(None, "head"),
            P(None, "head"),
        ),
        out_specs=(
            P("dp", "ctx", "head"),
            P("dp", "ctx", None),
            P("dp", "ctx", None),
            P(("dp", "ctx"), "head"),
            P(("dp", "ctx"), "head"),
        ),
        check_vma=False,
    )
```

profile of v0, /device:TPU:16, one launch (start us, length us, event | category | flops | bytes accessed | tf_op | source)
XLA Modules:
  0.0 362.8 jit_solution(10523931534086377642)
XLA Ops:
  7.3 1.1 copy.47
  8.4 1.1 copy.46
  9.5 0.7 pad_maximum_fusion.1
  10.3 1.3 reduce_max.9
  11.6 1.3 fusion.16
  14.2 1.1 convolution_convert_fusion.3
  16.0 34.6 %all_gather.7 = f32[8,1024]{1,0:T(8,128)S(1)} all-gather(f32[8,128]{1,0:T(8,128)S(1)} %pad_maximum_fusion.4), channel_id=1, replica_groups=mesh['dp'=8,'ctx'=8,'head'=16] {'ctx'}, dimensions={1}, use_global_device_ids=true | all-gather | bytes 36864 | tf_op jit(solution)/shard_map/all_gather | solution.py:18
  50.6 27.9 %all-gather.2.cloned.1.call-done = bf16[4,1024,320]{1,2,0:T(8,128)(2,1)} async-done(((bf16[4,128,320]{1,2,0:T(8,128)(2,1)}), bf16[4,1024,320]{1,2,0:T(8,128)(2,1)}) %all-gather.2.cloned.1.call-update) | async-done | bytes 2621456 | tf_op jit(solution)/shard_map/all_gather | solution.py:18
  78.5 13.9 %conditional.1 = (bf16[4,1024,192]{1,2,0:T(8,128)(2,1)S(1)}, f32[4,128,192]{1,2,0:T(8,128)S(1)}, f32[4,128,128]{2,1,0:T(8,128)S(1)}) conditional(s32[]{:T(128)} %convert_element_type.79, (s32[1,128]{1,0:T(1,128)S(1)}, s32[1,1024]{1,0:T(1,128)S(1)}, bf16[4,1024,320]{1,2,0:T(8,128)(2,1)}, bf16[4,128,192]{1,2,0:T(8,128)(2,1)S(1)}, ...), branch_computations={%region_3.4_spmd, %region_4.5_spmd} | conditional | flops 876740608 | bytes 35099244 | solution.py:107
  78.7 2.5 select_exponential_fusion
  81.3 4.5 %copy.44 = bf16[4,1024,320]{2,1,0:T(8,128)(2,1)} copy(bf16[4,1024,320]{1,2,0:T(8,128)(2,1)} %get-tuple-element.21) | data formatting | bytes 5242880 | tf_op jit(solution)/shard_map
  85.8 2.4 fusion.3
  88.2 2.7 multiply_convert_fusion
  92.4 0.7 copy-done.7
  93.1 1.4 fusion.7
  94.5 1.1 copy.52
  95.6 0.7 copy-done.2
  96.8 1.1 pad_maximum_fusion
  97.9 1.3 copy.54
  99.3 9.8 %all-to-all-start.1 = ((bf16[64,8,1024]{2,1,0:T(8,128)(2,1)}), bf16[64,8,1024]{2,1,0:T(8,128)(2,1)S(1)}, u32[]{:S(2)}, u32[]{:S(2)}) async-start(bf16[64,8,1024]{2,1,0:T(8,128)(2,1)} %bitcast.73), calls=%async_computation.1 | async-start | bytes 2097152 | tf_op jit(solution)/shard_map/all_to_all | solution.py:32
  109.5 1.5 copy.51
  111.0 0.9 slice_reduce_fusion
  112.2 0.7 fusion.20
  112.9 0.7 fusion.11
  113.7 24.2 %all-to-all-done.1 = bf16[64,8,1024]{2,1,0:T(8,128)(2,1)S(1)} async-done(((bf16[64,8,1024]{2,1,0:T(8,128)(2,1)}), bf16[64,8,1024]{2,1,0:T(8,128)(2,1)S(1)}, u32[]{:S(2)}, u32[]{:S(2)}) %all-to-all-start.1) | async-done | bytes 1048608 | tf_op jit(solution)/shard_map/all_to_all | solution.py:32
  137.8 5.1 %all-to-all-start = ((bf16[8,4,128,192]{2,3,1,0:T(8,128)(2,1)}), bf16[8,4,128,192]{2,3,1,0:T(8,128)(2,1)S(1)}, u32[]{:S(2)}, u32[]{:S(2)}) async-start(bf16[8,4,128,192]{2,3,1,0:T(8,128)(2,1)} %copy.51), calls=%async_computation | async-start | bytes 3145728 | tf_op jit(solution)/shard_map/all_to_all | solution.py:32
  143.6 207.3 %all-reduce.2.cloned.1.call-done = bf16[73728]{0:T(1024)(128)(2,1)} async-done(((bf16[73728]{0:T(1024)(128)(2,1)}), bf16[73728]{0:T(1024)(128)(2,1)}) %all-reduce.2.cloned.1.call-update) | async-done | bytes 147472 | tf_op jit(solution)/shard_map/psum | solution.py:38
  350.9 0.7 slice_convert_fusion.1
  351.7 0.7 copy.56
  352.4 0.9 slice_convert_fusion
  353.3 0.7 reshape.119
  355.1 0.8 copy.55
  (56 shorter events, 5.5 us)
Async XLA Ops:
  7.2 7.0 %copy-start = (bf16[512,512]{1,0:T(8,128)(2,1)S(1)}, bf16[512,512]{1,0:T(8,128)(2,1)}, u32[]{:S(2)}) copy-start(bf16[512,512]{1,0:T(8,128)(2,1)} %param.18) | copy-start | bytes 1572868
  7.2 8.3 %copy-start.6 = (bf16[1,128,512]{2,1,0:T(8,128)(2,1)S(1)}, bf16[1,128,512]{2,1,0:T(8,128)(2,1)}, u32[]{:S(2)}) copy-start(bf16[1,128,512]{2,1,0:T(8,128)(2,1)} %param.11) | copy-start | bytes 393220
  7.2 8.3 %copy-start.4 = (bf16[512,512]{1,0:T(8,128)(2,1)S(1)}, bf16[512,512]{1,0:T(8,128)(2,1)}, u32[]{:S(2)}) copy-start(bf16[512,512]{1,0:T(8,128)(2,1)} %param.19) | copy-start | bytes 1572868
  7.2 8.6 %copy-start.11 = (bf16[1,128,512]{2,1,0:T(8,128)(2,1)S(1)}, bf16[1,128,512]{2,1,0:T(8,128)(2,1)}, u32[]{:S(2)}) copy-start(bf16[1,128,512]{2,1,0:T(8,128)(2,1)} %param.15) | copy-start | bytes 393220
  7.2 71.3 %all-gather.2.cloned.1.call-start = ((), (), s32[]{:S(2)}) async-start(), calls=%async_computation.2 | async-start | bytes 2949120 | tf_op jit(solution)/shard_map/all_gather | solution.py:18
  8.4 7.6 %copy-start.14 = (f32[1,4,128]{2,1,0:T(4,128)S(1)}, f32[1,4,128]{2,1,0:T(4,128)}, u32[]{:S(2)}) copy-start(f32[1,4,128]{2,1,0:T(4,128)} %param.16) | copy-start | bytes 6148
  8.4 42.2 %copy-start.13 = (bf16[1,128,64]{1,2,0:T(8,128)(2,1)S(1)}, bf16[1,128,64]{1,2,0:T(8,128)(2,1)}, u32[]{:S(2)}) copy-start(bf16[1,128,64]{1,2,0:T(8,128)(2,1)} %param.12) | copy-start | bytes 49156
  9.5 69.0 %copy-start.12 = (s32[1,1024]{1,0:T(1,128)S(1)}, s32[1,1024]{1,0:T(1,128)}, u32[]{:S(2)}) copy-start(s32[1,1024]{1,0:T(1,128)} %param.17) | copy-start | bytes 12292
  78.5 2.8 copy-start.8
  88.1 2.7 copy-start.1
  90.8 0.9 copy-start.9
  92.4 0.7 copy-start.7
  93.1 1.4 copy-start.10
  95.5 0.7 copy-start.2
  99.3 38.6 %all-to-all-start.1 = ((bf16[64,8,1024]{2,1,0:T(8,128)(2,1)}), bf16[64,8,1024]{2,1,0:T(8,128)(2,1)S(1)}, u32[]{:S(2)}, u32[]{:S(2)}) async-start(bf16[64,8,1024]{2,1,0:T(8,128)(2,1)} %bitcast.73), calls=%async_computation.1 | async-start | bytes 2097152 | tf_op jit(solution)/shard_map/all_to_all | solution.py:32
  109.5 3.4 copy-start.3
  109.5 3.4 copy-start.5
  137.8 217.0 %all-to-all-start = ((bf16[8,4,128,192]{2,3,1,0:T(8,128)(2,1)}), bf16[8,4,128,192]{2,3,1,0:T(8,128)(2,1)S(1)}, u32[]{:S(2)}, u32[]{:S(2)}) async-start(bf16[8,4,128,192]{2,3,1,0:T(8,128)(2,1)} %copy.51), calls=%async_computation | async-start | bytes 3145728 | tf_op jit(solution)/shard_map/all_to_all | solution.py:32
  142.9 208.0 %all-reduce.2.cloned.1.call-start = ((), (), s32[]{:S(2)}) async-start(), calls=%async_computation.3 | async-start | bytes 294912 | tf_op jit(solution)/shard_map/psum | solution.py:38
Sparse Core Ops, SparseCore 0:
  10.6 67.8 all-gather.1
  147.8 203.0 all-reduce.1
where the time goes:
time: 364 us; the launch traced here: 363 us
  waiting for transfers between devices  259 us (71%)
  blocking collectives  34.6 us (10%)
  local copies, waits for them, and re-layouts  16.4 us (5%)
  between operations  15.6 us (4%)
  starting transfers between devices  14.9 us (4%)
  matrix products  13.4 us (4%)
  other arithmetic  8.41 us (2%)
    psum x1, waiting for transfers between devices, together(): so_far = lax.psum(line, axis)  207 us
    all_gather x1, blocking collectives, in_one_piece(): lax.all_gather(both, axis, axis=dim, tiled=True)  34.6 us
    all_gather x1, waiting for transfers between devices, in_one_piece(): lax.all_gather(both, axis, axis=dim, tiled=True)  27.9 us
    all_to_all x2, waiting for transfers between devices, sent_and_summed(): parts = lax.all_to_all(split_up(shard, dim, peers), axis, 0, 0, tiled=True)  24.2 us
    all_to_all x2, starting transfers between devices, sent_and_summed(): parts = lax.all_to_all(split_up(shard, dim, peers), axis, 0, 0, tiled=True)  14.8 us
  transfers between devices with their start and end apart: 4, of which 3 were waited for; matrix products, arithmetic and copies ran while one was open for 4% of the time, Pallas kernels for 0%

commit v1 on v0

v1 whole, which is shorter than its diff:
```python
import math

import jax
import jax.numpy as jnp
from jax import lax
from jax.experimental import pallas as pl
from jax.experimental.pallas import tpu as pltpu
from jax.sharding import PartitionSpec as P

DL = 512
DR = 64
DN = 128
DV = 128
HPD = 4
ROWS = 128
NY = 8
NX = 8
NZ = 4
SL = ROWS // NX
GW = 640
MASKED = -1e30
SCALE = 1.0 / math.sqrt(DN + DR)
MESH = pl.DeviceIdType.MESH
F32 = jnp.float32
BF16 = jnp.bfloat16

OFFS = (0, -1, 1, -2, 2, -3, 3, 4)
GROUPS = ((0, 1), (1, 3), (3, 5), (5, 7), (7, 8))


def wrap(v, n):
    return lax.rem(v + 2 * n, n)


def dot(a, b, ca, cb):
    return lax.dot_general(a, b, (((ca,), (cb,)), ((), ())), preferred_element_type=F32)


def kernel(
    lat_ref, rope_ref, q_ref, go_ref, ao_ref, lse_ref, pos_ref, wuk_ref, wuv_ref,
    dq_out, gl_out, gr_out, guk_out, guv_out,
    lat_all, rope_all, qh, gh, delta, dq_acc, dkv_all, glb, xl, xr,
    ysend, yrecv, zs, zr, axr,
    wgb, wgc, wa, wb, wa_in, wb_in, wa2, wb2, wa2_in, wb2_in,
    ag_s, ag_r, xl_s, xl_r, xr_s, xr_r, y_s, y_r, z_sem, ax_s, ax_r,
    c_s, c_r, wy_s, wy_r, wz_s, wz_r, wy2_s, wy2_r, wz2_s, wz2_r,
):
    dp = lax.axis_index("dp")
    y = lax.axis_index("ctx")
    head = lax.axis_index("head")
    c, zl = lax.rem(dp, 2), dp // 2
    x, zh = head // 2, lax.rem(head, 2)

    def to_y(v):
        return {"ctx": wrap(v, NY)}

    def to_x(v):
        return {"head": wrap(v, NX) * 2 + zh}

    def to_z(v):
        return {"dp": wrap(v, NZ) * 2 + c}

    other_core = {"dp": zl * 2 + (1 - c)}
    other_half = {"head": x * 2 + (1 - zh)}

    barrier = pltpu.get_barrier_semaphore()
    peers = [to_y(y + 1), to_y(y - 1), to_x(x + 1), to_x(x - 1)]
    peers += [to_z(zl + d) for d in range(1, NZ)] + [other_core, other_half]
    for peer in peers:
        pl.semaphore_signal(barrier, inc=1, device_id=peer, device_id_type=MESH)

    started = []

    def send(src, dst, s_sem, r_sem, device):
        copy = pltpu.make_async_remote_copy(
            src_ref=src, dst_ref=dst, send_sem=s_sem, recv_sem=r_sem,
            device_id=device, device_id_type=MESH,
        )
        copy.start()
        started.append(copy)
        return copy

    lat_all[y] = lat_ref[0]
    rope_all[y] = jnp.concatenate([rope_ref[0, 0:64, :], rope_ref[0, 64:128, :]], axis=1)
    for h in range(HPD):
        qh[h] = q_ref[0, :, 192 * h : 192 * h + 192]
        g = go_ref[0, :, 128 * h : 128 * h + 128]
        gh[h] = g
        prod = g.astype(F32) * ao_ref[0, :, 128 * h : 128 * h + 128].astype(F32)
        delta[h : h + 1, :] = jnp.sum(prod.T, axis=0, keepdims=True)

    pl.semaphore_wait(barrier, len(peers))

    def ag_parts(block):
        return (
            lat_all.at[block, pl.ds(0, 64)],
            lat_all.at[block, pl.ds(64, 64)],
            rope_all.at[block],
        )

    ag = {}

    def ag_step(k):
        for part in range(3):
            for way, sign in ((0, 1), (1, -1)):
                if k == 3 and (part == 0) != (way == 0):
                    continue
                if k > 0:
                    ag[way, k - 1, part].wait_recv()
                ref = ag_parts(wrap(y - sign * k, NY))[part]
                ag[way, k, part] = send(
                    ref, ref, ag_s.at[way, k, part], ag_r.at[way, k, part], to_y(y + sign)
                )

    def ag_rest(k):
        for part in range(3):
            for way in (0, 1):
                if k == 3 and (part == 0) != (way == 0):
                    ag[way, k - 1, part].wait_recv()

    pos_q = pos_ref[:, pl.ds(pl.multiple_of(y * ROWS, ROWS), ROWS)].astype(F32)

    def compute(group):
        lo, hi = GROUPS[group]
        blocks = [wrap(y + OFFS[r], NY) for r in range(lo, hi)]
        n = len(blocks)

        def joined(parts):
            return parts[0] if n == 1 else jnp.concatenate(parts, axis=0)

        lat = joined([lat_all[b] for b in blocks])
        ropes, masks = [], []
        for b in blocks:
            packed = rope_all[b]
            ropes += [packed[:, 0:64], packed[:, 64:128]]
            pos_k = pos_ref[:, pl.ds(pl.multiple_of(b * ROWS, ROWS), ROWS)].astype(F32)
            masks.append(jnp.broadcast_to(pos_k, (ROWS, ROWS)).T)
        rope = jnp.concatenate(ropes, axis=0)
        allowed = joined(masks) <= pos_q
        keys = dot(lat, wuk_ref[...], 1, 0).astype(BF16)
        values = dot(lat, wuv_ref[...], 1, 0).astype(BF16)
        rope_grad = None
        dks, dvs = [], []
        for h in range(HPD):
            kh = jnp.concatenate([keys[:, 128 * h : 128 * h + 128], rope], axis=1)
            vh = values[:, 128 * h : 128 * h + 128]
            q, g = qh[h], gh[h]
            scores = dot(kh, q, 1, 1) * SCALE
            dots = dot(vh, g, 1, 1)
            w = jnp.exp(jnp.where(allowed, scores - lse_ref[0, h : h + 1, :], MASKED))
            sg = (w * (dots - delta[h : h + 1, :]) * SCALE).astype(BF16)
            dk = dot(sg, q, 1, 0)
            dv = dot(w.astype(BF16), g, 1, 0)
            dq = dot(sg, kh, 0, 0)
            if group == 0:
                dq_acc[h] = dq
            else:
                dq_acc[h] += dq
            part = dk[:, 128:192]
            rope_grad = part if rope_grad is None else rope_grad + part
            dks.append(dk[:, 0:128].astype(BF16))
            dvs.append(dv.astype(BF16))
        dkn = jnp.concatenate(dks, axis=1)
        dvn = jnp.concatenate(dvs, axis=1)
        for i, b in enumerate(blocks):
            dkv_all[b, :, 0:512] = dkn[128 * i : 128 * i + 128]
            dkv_all[b, :, 512:1024] = dvn[128 * i : 128 * i + 128]
        gl = dot(dkn, wuk_ref[...], 1, 1) + dot(dvn, wuv_ref[...], 1, 1)
        whole = jnp.concatenate([gl, rope_grad, jnp.zeros_like(rope_grad)], axis=1).astype(BF16)
        for i in range(n):
            for s in range(NX):
                at = 128 * i + SL * s
                glb[s, lo + i] = whole[at : at + SL]

    arms = {}

    def hops(group, way):
        return 4 if (group + way) % 2 == 0 else 3

    def chain(group, k):
        lo, hi = GROUPS[group]
        for way, sign, slots, s_sem, r_sem in (
            (0, -1, xl, xl_s, xl_r),
            (1, 1, xr, xr_s, xr_r),
        ):
            length = hops(group, way)
            if k >= length:
                continue
            dest = wrap(x + sign * (length - k), NX)
            own = glb.at[dest, lo:hi]
            src = own
            if k > 0:
                arms[group, way, k - 1].wait_recv()
                src = slots.at[k - 1, lo:hi]
                src[...] = (src[...].astype(F32) + own[...].astype(F32)).astype(BF16)
            arms[group, way, k] = send(
                src, slots.at[k, lo:hi], s_sem.at[group, k], r_sem.at[group, k], to_x(x + sign)
            )

    y_copies = {}

    def chain_end(group):
        lo, hi = GROUPS[group]
        last = (hops(group, 0) - 1, hops(group, 1) - 1)
        for way in (0, 1):
            arms[group, way, last[way]].wait_recv()
        total = (
            glb[x, lo:hi].astype(F32)
            + xl[last[0], lo:hi].astype(F32)
            + xr[last[1], lo:hi].astype(F32)
        )
        ysend[lo:hi] = total.astype(BF16)
        for r in range(lo, hi):
            if r > 0:
                y_copies[r] = send(
                    ysend.at[r], yrecv.at[r], y_s.at[r], y_r.at[r], to_y(y + OFFS[r])
                )

    core_copies = {}

    def weight_rows(z):
        lat = lat_all[:, :, 128 * z : 128 * z + 128].reshape(NY * ROWS, 128)
        rows = dot(lat, dkv_all[...].reshape(NY * ROWS, 1024), 0, 0)
        for half in range(2):
            wgb[half, z] = rows[64 * half : 64 * half + 64].reshape(NY, 8, 1024).astype(BF16)
        core_copies[z] = send(wgb.at[1 - c, z], wgc.at[z], c_s.at[z], c_r.at[z], other_core)

    ag_step(0)
    compute(0)
    chain(0, 0)
    ag_step(1)
    compute(1)
    chain(1, 0)
    chain(0, 1)
    ag_step(2)
    compute(2)
    chain(2, 0)
    chain(1, 1)
    chain(0, 2)
    ag_step(3)
    ag_rest(3)
    compute(3)
    chain(3, 0)
    chain(2, 1)
    chain(1, 2)
    chain(0, 3)
    ag[0, 3, 0].wait_recv()
    ag[1, 3, 1].wait_recv()
    ag[1, 3, 2].wait_recv()
    compute(4)
    chain(4, 0)
    chain(3, 1)
    chain(2, 2)
    chain(1, 3)
    chain_end(0)
    weight_rows(0)
    weight_rows(1)
    chain(4, 1)
    chain(3, 2)
    chain(2, 3)
    chain_end(1)
    weight_rows(2)
    weight_rows(3)
    chain(4, 2)
    chain(3, 3)
    chain_end(2)

    for z in range(NZ):
        core_copies[z].wait_recv()
        both = wgb[c, z].astype(F32) + wgc[z].astype(F32)
        both = both.astype(BF16)
        wa[:, z] = both[:, :, 0:512]
        wb[z] = both[:, :, 512:1024]
    wa_copies, wb_copies = [], []
    for d in (4, 3, 5, 2, 6, 1, 7):
        at = wrap(y + d, NY)
        wa_copies.append(
            send(wa.at[at], wa_in.at[d], wy_s.at[d], wy_r.at[d], to_y(y + d))
        )
    for d in (2, 1, 3):
        at = wrap(zl + d, NZ)
        wb_copies.append(
            send(wb.at[at], wb_in.at[d], wz_s.at[d], wz_r.at[d], to_z(zl + d))
        )
    chain(4, 3)
    chain_end(3)
    chain_end(4)

    for r in range(1, NY):
        y_copies[r].wait_recv()
    total = ysend[0].astype(F32)
    for r in range(1, NY):
        total += yrecv[r].astype(F32)
    zs[...] = total.astype(BF16)
    z_copy = send(zs, zr, z_sem.at[0], z_sem.at[1], other_half)

    for h in range(HPD):
        dq_out[0, :, 192 * h : 192 * h + 192] = dq_acc[h].astype(BF16)

    for copy in wb_copies:
        copy.wait_recv()
    total = wb[zl].astype(F32)
    for d in range(1, NZ):
        total += wb_in[d].astype(F32)
    wb2[...] = total.astype(BF16)
    wb2_copies = []
    for d in (4, 3, 5, 2, 6, 1, 7):
        at = wrap(y + d, NY)
        wb2_copies.append(
            send(wb2.at[at], wb2_in.at[d], wy2_s.at[d], wy2_r.at[d], to_y(y + d))
        )
    z_copy.wait_recv()
    axr[x] = (zs[...].astype(F32) + zr[...].astype(F32)).astype(BF16)
    ax_copies = []
    for d in (4, 3, 5, 2, 6, 1, 7):
        ax_copies.append(
            send(axr.at[x], axr.at[x], ax_s.at[d], ax_r.at[d], to_x(x + d))
        )
    for copy in wa_copies:
        copy.wait_recv()
    total = wa[y].astype(F32)
    for d in range(1, NY):
        total += wa_in[d].astype(F32)
    wa2[...] = total.astype(BF16)
    wa2_copies = []
    for d in (2, 1, 3):
        at = wrap(zl + d, NZ)
        wa2_copies.append(
            send(wa2.at[at], wa2_in.at[d], wz2_s.at[d], wz2_r.at[d], to_z(zl + d))
        )
    for copy in wb2_copies:
        copy.wait_recv()
    total = wb2[y].astype(F32)
    for d in range(1, NY):
        total += wb2_in[d].astype(F32)
    guv_out[...] = total.astype(BF16)
    for copy in wa2_copies:
        copy.wait_recv()
    total = wa2[zl].astype(F32)
    for d in range(1, NZ):
        total += wa2_in[d].astype(F32)
    guk_out[...] = total.astype(BF16)
    for copy in ax_copies:
        copy.wait_recv()
    for s in range(NX):
        gl_out[0, SL * s : SL * s + SL, :] = axr[s, :, 0:512].astype(F32)
        gr_out[0, SL * s : SL * s + SL, :] = axr[s, :, 512:576].astype(F32)
    for copy in started:
        copy.wait_send()


def on_device(latent, rope, query, grad_out, attn_out, lse, positions, w_uk, w_uv):
    vmem = pl.BlockSpec(memory_space=pltpu.VMEM)
    dma = pltpu.SemaphoreType.DMA
    shapes = [
        pltpu.VMEM((NY, ROWS, DL), BF16),
        pltpu.VMEM((NY, 64, 128), BF16),
        pltpu.VMEM((HPD, ROWS, 192), BF16),
        pltpu.VMEM((HPD, ROWS, DV), BF16),
        pltpu.VMEM((8, ROWS), F32),
        pltpu.VMEM((HPD, ROWS, 192), F32),
        pltpu.VMEM((NY, ROWS, 1024), BF16),
        pltpu.VMEM((NX, NY, SL, GW), BF16),
        pltpu.VMEM((4, NY, SL, GW), BF16),
        pltpu.VMEM((4, NY, SL, GW), BF16),
        pltpu.VMEM((NY, SL, GW), BF16),
        pltpu.VMEM((NY, SL, GW), BF16),
        pltpu.VMEM((SL, GW), BF16),
        pltpu.VMEM((SL, GW), BF16),
        pltpu.VMEM((NX, SL, GW), BF16),
        pltpu.VMEM((2, NZ, NY, 8, 1024), BF16),
        pltpu.VMEM((NZ, NY, 8, 1024), BF16),
        pltpu.VMEM((NY, NZ, 8, 512), BF16),
        pltpu.VMEM((NZ, NY, 8, 512), BF16),
        pltpu.VMEM((NY, NZ, 8, 512), BF16),
        pltpu.VMEM((NZ, NY, 8, 512), BF16),
        pltpu.VMEM((NZ, 8, 512), BF16),
        pltpu.VMEM((NY, 8, 512), BF16),
        pltpu.VMEM((NZ, 8, 512), BF16),
        pltpu.VMEM((NY, 8, 512), BF16),
        dma((2, 4, 3)), dma((2, 4, 3)),
        dma((5, 4)), dma((5, 4)), dma((5, 4)), dma((5, 4)),
        dma((NY,)), dma((NY,)), dma((2,)), dma((NX,)), dma((NX,)),
        dma((NZ,)), dma((NZ,)),
        dma((NY,)), dma((NY,)), dma((NZ,)), dma((NZ,)),
        dma((NY,)), dma((NY,)), dma((NZ,)), dma((NZ,)),
    ]
    return pl.pallas_call(
        kernel,
        out_shape=(
            jax.ShapeDtypeStruct((1, ROWS, HPD * 192), BF16),
            jax.ShapeDtypeStruct((1, ROWS, DL), F32),
            jax.ShapeDtypeStruct((1, ROWS, DR), F32),
            jax.ShapeDtypeStruct((8, 512), BF16),
            jax.ShapeDtypeStruct((8, 512), BF16),
        ),
        in_specs=[vmem] * 9,
        out_specs=(vmem,) * 5,
        scratch_shapes=shapes,
        compiler_params=pltpu.CompilerParams(
            collective_id=0, has_side_effects=True, vmem_limit_bytes=60 * 1024 * 1024
        ),
    )(latent, rope, query, grad_out, attn_out, lse, positions, w_uk, w_uv)


def solution(mesh):
    return jax.shard_map(
        on_device,
        mesh=mesh,
        in_specs=(
            P("dp", "ctx", None),
            P("dp", "ctx", None),
            P("dp", "ctx", "head"),
            P("dp", "ctx", "head"),
            P("dp", "ctx", "head"),
            P("dp", "head", "ctx"),
            P("dp", None),
            P(None, "head"),
            P(None, "head"),
        ),
        out_specs=(
            P("dp", "ctx", "head"),
            P("dp", "ctx", None),
            P("dp", "ctx", None),
            P(("dp", "ctx"), "head"),
            P(("dp", "ctx"), "head"),
        ),
        check_vma=False,
    )
```

time: 364 us -> 80.8 us (0.22)
  the two profiles are of different devices: /device:TPU:16 before, /device:TPU:2 now
where the time goes in v1:
time: 80.8 us; the launch traced here: 80.3 us
  Pallas kernels  73.1 us (90%)
  local copies, waits for them, and re-layouts  6.64 us (8%)
    pallas_call x1, Pallas kernels, on_device(): pl.pallas_call(kernel, out_shape=(jax.ShapeDtypeStruct((1, ROWS, HPD * 19...  73.1 us
    unnamed x11, local copies, waits for them, and re-layouts  5.06 us

profile of v1, /device:TPU:2, one launch (start us, length us, event | category | flops | bytes accessed | tf_op | source)
XLA Modules:
  0.0 80.3 jit_solution(7873826498546313516)
XLA Ops:
  0.6 1.4 %copy.14.rope_ref = bf16[1,128,64]{2,1,0:T(8,128)(2,1)} copy(bf16[1,128,64]{1,2,0:T(8,128)(2,1)} %param.10) | data formatting | bytes 32768 | tf_op args[1]
  2.1 73.1 %shard_map.128 = (bf16[1,128,768]{2,1,0:T(8,128)(2,1)}, f32[1,128,512]{2,1,0:T(8,128)}, f32[1,128,64]{2,1,0:T(8,128)}, bf16[8,512]{1,0:T(8,128)(2,1)}, bf16[8,512]{1,0:T(8,128)(2,1)}) custom-call(bf16[1,128,512]{2,1,0:T(8,128)(2,1)} %lat_ref.1, bf16[1,128,64]{2,1,0:T(8,128)(2,1)} %copy.14.rope_ref, bf16[1,128,768]{2,1,0:T(8,128)(2,1)} %q_ref.1, ...), custom_call_target="tpu_custom_call" | custom-call | tf_op jit(solution)/shard_map/pallas_call | solution.py:388
  75.1 0.0 copy-start
  75.1 1.6 %copy.15 = f32[1,128,64]{1,2,0:T(8,128)} copy(f32[1,128,64]{2,1,0:T(8,128)} %get-tuple-element.7) | data formatting | bytes 65536 | tf_op jit(solution)/shard_map/pallas_call | solution.py:388
  76.7 1.6 %copy.20 = bf16[1,128,768]{2,1,0:T(8,128)(2,1)} copy(bf16[1,128,768]{2,1,0:T(8,128)(2,1)} %get-tuple-element.15) | data formatting | bytes 393216
  78.3 0.0 copy-done
  78.3 0.0 copy-start.2
  78.3 0.7 copy.21
  79.0 0.0 copy-done.2
  79.0 0.0 copy-start.1
  79.0 0.6 copy.22
  79.6 0.1 copy-done.1
  79.7 0.6 copy.23
Async XLA Ops:
  75.1 3.2 %copy-start = (f32[1,128,512]{2,1,0:T(8,128)S(1)}, f32[1,128,512]{2,1,0:T(8,128)}, u32[]{:S(2)}) copy-start(f32[1,128,512]{2,1,0:T(8,128)} %get-tuple-element.16) | copy-start | bytes 786436
  78.3 0.7 copy-start.2
  79.0 0.7 copy-start.1

commit v2 on v1

v2 whole, which is shorter than its diff:
```python
import math

import jax
import jax.numpy as jnp
from jax import lax
from jax.experimental import pallas as pl
from jax.experimental.pallas import tpu as pltpu
from jax.sharding import PartitionSpec as P

DL = 512
DR = 64
DN = 128
DV = 128
HPD = 4
ROWS = 128
NY = 8
NX = 8
NZ = 4
SL = ROWS // NX
GR = 72
QR = 144
MASKED = -1e30
SCALE = 1.0 / math.sqrt(DN + DR)
VMEM_LIMIT = 40 * 1024 * 1024
MESH = pl.DeviceIdType.MESH
F32 = jnp.float32
BF16 = jnp.bfloat16

OFFS = (0, -1, 1, -2, 2, -3, 3, 4)
GROUPS = ((0, 1), (1, 3), (3, 5), (5, 7), (7, 8))


def wrap(v, n):
    return lax.rem(v + 2 * n, n)


def dot(a, b, ca, cb):
    return lax.dot_general(a, b, (((ca,), (cb,)), ((), ())), preferred_element_type=F32)


def kernel(
    lat_hbm, rope_hbm, lse_hbm, pos_hbm, q_hbm, go_hbm, ao_hbm, wuk_hbm, wuv_hbm,
    dq_out, ax_out, guk_out, guv_out,
    lat_ref, rope_ref, lse_ref, pos_ref, q_ref, go_ref, ao_ref, wuk_ref, wuv_ref,
    kv_all, qh, gh, delta, dq_acc, dkv_all, glb, xl, xr, ysend, yrecv, zs, zr, axr,
    wgb, wgc, wa, wb, wa_in, wb_in, wa2, wb2, wa2_in, wb2_in,
    in_sem, ag_s, ag_r, agx_s, agx_r, xl_s, xl_r, xr_s, xr_r, y_sem, z_sem, ax_sem,
    c_sem, wy_sem, wz_sem, wy2_sem, wz2_sem,
):
    dp = lax.axis_index("dp")
    y = lax.axis_index("ctx")
    head = lax.axis_index("head")
    c, zl = lax.rem(dp, 2), dp // 2
    x, zh = head // 2, lax.rem(head, 2)
    side = lax.rem(x, 2)

    def to_y(v):
        return {"ctx": wrap(v, NY)}

    def to_x(v):
        return {"head": wrap(v, NX) * 2 + zh}

    def to_z(v):
        return {"dp": wrap(v, NZ) * 2 + c}

    other_core = {"dp": zl * 2 + (1 - c)}
    other_half = {"head": x * 2 + (1 - zh)}

    barrier = pltpu.get_barrier_semaphore()
    peers = [to_y(y + 1), to_y(y - 1), to_x(x + 1), to_x(x - 1)]
    peers += [to_z(zl + d) for d in range(1, NZ)] + [other_core, other_half]
    for peer in peers:
        pl.semaphore_signal(barrier, inc=1, device_id=peer, device_id_type=MESH)

    loads = []
    for i, (a, b) in enumerate(
        (
            (lat_hbm, lat_ref), (rope_hbm, rope_ref), (q_hbm, q_ref), (go_hbm, go_ref),
            (ao_hbm, ao_ref), (lse_hbm, lse_ref), (pos_hbm, pos_ref), (wuk_hbm, wuk_ref),
            (wuv_hbm, wuv_ref),
        )
    ):
        loads.append(pltpu.make_async_copy(a, b, in_sem.at[i]))
        loads[i].start()

    def copy_of(src, dst, s_sem, r_sem, device):
        return pltpu.make_async_remote_copy(
            src_ref=src, dst_ref=dst, send_sem=s_sem, recv_sem=r_sem,
            device_id=device, device_id_type=MESH,
        )

    def send(src, dst, s_sem, r_sem, device):
        copy = copy_of(src, dst, s_sem, r_sem, device)
        copy.start()
        return copy

    loads[0].wait()
    loads[1].wait()
    for t in range(4):
        for ct in range(4):
            kv_all[y, t, 32 * ct : 32 * ct + 32, :] = lat_ref[
                0, 32 * t : 32 * t + 32, 128 * ct : 128 * ct + 128
            ]
        kv_all[y, t, 128:144, :] = rope_ref[0, 16 * t : 16 * t + 16, :]

    pl.semaphore_wait(barrier, len(peers))

    ag, agx = {}, {}

    def ag_step(k):
        for part in range(2):
            for way, sign in ((0, 1), (1, -1)):
                if k == 4 and part != way:
                    continue
                if k > 0:
                    ag[way, k - 1, part].wait_recv()
                ref = kv_all.at[wrap(y - sign * k, NY), 2 * side + part]
                if k < 3 or (k == 3 and part == way):
                    ag[way, k, part] = send(
                        ref, ref, ag_s.at[way], ag_r.at[way, k, part], to_y(y + sign)
                    )
                if k > 0:
                    r = 2 * k - 1 + way if k < 4 else 7
                    agx[r, part] = send(
                        ref, ref, agx_s.at[part], agx_r.at[r, part], to_x(x + 1 - 2 * part)
                    )

    def agx_wait(group):
        for r in range(*GROUPS[group]):
            for part in range(2):
                agx[r, part].wait_recv()

    def prepare():
        for load in loads[2:]:
            load.wait()
        for h in range(HPD):
            qh[h] = q_ref[0, :, 192 * h : 192 * h + 192]
            g = go_ref[0, :, 128 * h : 128 * h + 128]
            gh[h] = g
            prod = g.astype(F32) * ao_ref[0, :, 128 * h : 128 * h + 128].astype(F32)
            delta[h : h + 1, :] = jnp.sum(prod.T, axis=0, keepdims=True)

    def lat_of(b):
        quarters = [
            jnp.concatenate([kv_all[b, t, 32 * ct : 32 * ct + 32, :] for ct in range(4)], axis=1)
            for t in range(4)
        ]
        return jnp.concatenate(quarters, axis=0)

    def rope_of(b):
        return jnp.concatenate([kv_all[b, t, 128:144, :] for t in range(4)], axis=0).T

    def compute(group):
        pos_q = pos_ref[:, pl.ds(pl.multiple_of(y * ROWS, ROWS), ROWS)].astype(F32)
        lo, hi = GROUPS[group]
        blocks = [wrap(y + OFFS[r], NY) for r in range(lo, hi)]
        n = len(blocks)

        def joined(parts):
            return parts[0] if n == 1 else jnp.concatenate(parts, axis=0)

        masks = []
        for b in blocks:
            pos_k = pos_ref[:, pl.ds(pl.multiple_of(b * ROWS, ROWS), ROWS)].astype(F32)
            masks.append(jnp.broadcast_to(pos_k, (ROWS, ROWS)).T)
        lat = joined([lat_of(b) for b in blocks])
        rope = joined([rope_of(b) for b in blocks])
        allowed = joined(masks) <= pos_q
        keys = dot(lat, wuk_ref[...], 1, 0).astype(BF16)
        values = dot(lat, wuv_ref[...], 1, 0).astype(BF16)
        rope_grad = None
        dks, dvs = [], []
        for h in range(HPD):
            kh = jnp.concatenate([keys[:, 128 * h : 128 * h + 128], rope], axis=1)
            vh = values[:, 128 * h : 128 * h + 128]
            q, g = qh[h], gh[h]
            scores = dot(kh, q, 1, 1) * SCALE
            dots = dot(vh, g, 1, 1)
            w = jnp.exp(jnp.where(allowed, scores - lse_ref[0, h : h + 1, :], MASKED))
            sg = (w * (dots - delta[h : h + 1, :]) * SCALE).astype(BF16)
            dk = dot(sg, q, 1, 0)
            dv = dot(w.astype(BF16), g, 1, 0)
            dq = dot(sg, kh, 0, 0)
            if group == 0:
                dq_acc[h] = dq
            else:
                dq_acc[h] += dq
            part = dk[:, 128:192]
            rope_grad = part if rope_grad is None else rope_grad + part
            dks.append(dk[:, 0:128].astype(BF16))
            dvs.append(dv.astype(BF16))
        dkn = jnp.concatenate(dks, axis=1)
        dvn = jnp.concatenate(dvs, axis=1)
        for i, b in enumerate(blocks):
            dkv_all[b, :, 0:512] = dkn[128 * i : 128 * i + 128]
            dkv_all[b, :, 512:1024] = dvn[128 * i : 128 * i + 128]
        gl = (dot(dkn, wuk_ref[...], 1, 1) + dot(dvn, wuv_ref[...], 1, 1)).astype(BF16)
        for i in range(n):
            turned = rope_grad[128 * i : 128 * i + 128].T
            for s in range(NX):
                at = 128 * i + SL * s
                for ct in range(4):
                    glb[s, lo + i, 16 * ct : 16 * ct + 16, :] = gl[
                        at : at + SL, 128 * ct : 128 * ct + 128
                    ]
                glb[s, lo + i, 64:72, :] = turned[8 * s : 8 * s + 8].astype(BF16)

    arms = {}

    def hops(group, way):
        return 4 if (group + way) % 2 == 0 else 3

    def chain(group, k):
        lo, hi = GROUPS[group]
        for way, sign, slots, s_sem, r_sem in (
            (0, -1, xl, xl_s, xl_r),
            (1, 1, xr, xr_s, xr_r),
        ):
            length = hops(group, way)
            if k >= length:
                continue
            dest = wrap(x + sign * (length - k), NX)
            own = glb.at[dest, lo:hi]
            src = own
            if k > 0:
                arms[group, way, k - 1].wait_recv()
                src = slots.at[k - 1, lo:hi]
                src[...] = (src[...].astype(F32) + own[...].astype(F32)).astype(BF16)
            arms[group, way, k] = send(
                src, slots.at[k, lo:hi], s_sem.at[group], r_sem.at[group, k], to_x(x + sign)
            )

    def chain_end(group):
        lo, hi = GROUPS[group]
        last = (hops(group, 0) - 1, hops(group, 1) - 1)
        for way in (0, 1):
            arms[group, way, last[way]].wait_recv()
        total = (
            glb[x, lo:hi].astype(F32)
            + xl[last[0], lo:hi].astype(F32)
            + xr[last[1], lo:hi].astype(F32)
        )
        ysend[lo:hi] = total.astype(BF16)
        for r in range(lo, hi):
            if r > 0:
                send(ysend.at[r], yrecv.at[r], y_sem.at[0], y_sem.at[1], to_y(y + OFFS[r]))

    def weight_rows(z):
        lat = kv_all[:, :, 32 * z : 32 * z + 32, :].reshape(NY * ROWS, 128)
        rows = dot(lat, dkv_all[...].reshape(NY * ROWS, 1024), 0, 0)
        for half in range(2):
            wgb[half, z] = rows[64 * half : 64 * half + 64].reshape(NY, 8, 1024).astype(BF16)
        send(wgb.at[1 - c, z], wgc.at[z], c_sem.at[0], c_sem.at[1], other_core)

    def spread(src, dst, sem, n, me, to):
        order = (4, 3, 5, 2, 6, 1, 7) if n == 8 else (2, 1, 3)
        for d in order:
            send(src.at[wrap(me + d, n)], dst.at[d], sem.at[0], sem.at[1], to(me + d))

    def whole(ref, sem):
        return copy_of(ref, ref, sem.at[0], sem.at[1], other_half)

    def summed(own, got, n):
        total = own.astype(F32)
        for d in range(1, n):
            total += got[d].astype(F32)
        return total.astype(BF16)

    ag_step(0)
    prepare()
    compute(0)
    chain(0, 0)
    ag_step(1)
    ag_step(2)
    chain(0, 1)
    agx_wait(1)
    compute(1)
    chain(1, 0)
    ag_step(3)
    chain(0, 2)
    agx_wait(2)
    compute(2)
    chain(2, 0)
    ag_step(4)
    chain(1, 1)
    chain(0, 3)
    agx_wait(3)
    compute(3)
    chain(3, 0)
    chain(2, 1)
    chain(1, 2)
    agx_wait(4)
    compute(4)
    chain(4, 0)
    chain(3, 1)
    chain(2, 2)
    chain(1, 3)
    chain_end(0)
    weight_rows(0)
    weight_rows(1)
    chain(4, 1)
    chain(3, 2)
    chain(2, 3)
    chain_end(1)
    weight_rows(2)
    weight_rows(3)
    chain(4, 2)
    chain(3, 3)
    chain_end(2)
    for h in range(HPD):
        dq_out[0, :, 192 * h : 192 * h + 192] = dq_acc[h].astype(BF16)
    chain(4, 3)
    chain_end(3)
    chain_end(4)

    whole(wgc, c_sem).wait_recv()
    for z in range(NZ):
        both = (wgb[c, z].astype(F32) + wgc[z].astype(F32)).astype(BF16)
        wa[:, z] = both[:, :, 0:512]
        wb[z] = both[:, :, 512:1024]
    spread(wb, wb_in, wz_sem, NZ, zl, to_z)
    spread(wa, wa_in, wy_sem, NY, y, to_y)

    whole(yrecv.at[1:8], y_sem).wait_recv()
    zs[...] = summed(ysend[0], yrecv, NY)
    z_copy = send(zs, zr, z_sem.at[0], z_sem.at[1], other_half)

    whole(wb_in.at[1:4], wz_sem).wait_recv()
    wb2[...] = summed(wb[zl], wb_in, NZ)
    spread(wb2, wb2_in, wy2_sem, NY, y, to_y)

    z_copy.wait_recv()
    axr[x] = (zs[...].astype(F32) + zr[...].astype(F32)).astype(BF16)
    for d in (4, 3, 5, 2, 6, 1, 7):
        send(axr.at[x], axr.at[x], ax_sem.at[0], ax_sem.at[1], to_x(x + d))

    whole(wa_in.at[1:8], wy_sem).wait_recv()
    wa2[...] = summed(wa[y], wa_in, NY)
    spread(wa2, wa2_in, wz2_sem, NZ, zl, to_z)

    whole(wb2_in.at[1:8], wy2_sem).wait_recv()
    guv_out[...] = summed(wb2[y], wb2_in, NY)
    whole(wa2_in.at[1:4], wz2_sem).wait_recv()
    guk_out[...] = summed(wa2[zl], wa2_in, NZ)
    whole(axr.at[1:8], ax_sem).wait_recv()
    ax_out[...] = axr[...]

    for sem in (ag_s.at[0], ag_s.at[1], agx_s.at[0], agx_s.at[1]):
        copy_of(glb.at[1:8, 0:2], glb.at[1:8, 0:2], sem, sem, other_half).wait_send()
    for way, slots, s_sem in ((0, xl, xl_s), (1, xr, xr_s)):
        for group, (lo, hi) in enumerate(GROUPS):
            part = slots.at[0 : hops(group, way), lo:hi]
            copy_of(part, part, s_sem.at[group], s_sem.at[group], other_half).wait_send()
    for ref, sem in (
        (wgc, c_sem), (yrecv.at[1:8], y_sem), (zr, z_sem), (axr.at[1:8], ax_sem),
        (wb_in.at[1:4], wz_sem), (wa_in.at[1:8], wy_sem),
        (wb2_in.at[1:8], wy2_sem), (wa2_in.at[1:4], wz2_sem),
    ):
        whole(ref, sem).wait_send()


def finish(dq_ref, ax_ref, guk_ref, guv_ref, dq_out, gl_out, gr_out, guk_out, guv_out):
    dq_out[...] = dq_ref[...]
    for s in range(NX):
        for ct in range(4):
            gl_out[0, SL * s : SL * s + SL, 128 * ct : 128 * ct + 128] = ax_ref[
                s, 16 * ct : 16 * ct + 16, :
            ].astype(F32)
        gr_out[0, 8 * s : 8 * s + 8, :] = ax_ref[s, 64:72, :].astype(F32)
    guk_out[...] = guk_ref[...]
    guv_out[...] = guv_ref[...]


def on_device(latent, rope, query, grad_out, attn_out, lse, positions, w_uk, w_uv):
    vmem = pl.BlockSpec(memory_space=pltpu.VMEM)
    hbm = pl.BlockSpec(memory_space=pltpu.HBM)
    dma = pltpu.SemaphoreType.DMA
    shapes = [
        pltpu.VMEM((1, ROWS, DL), BF16),
        pltpu.VMEM((1, DR, ROWS), BF16),
        pltpu.VMEM((1, HPD, ROWS), F32),
        pltpu.VMEM((1, NY * ROWS), jnp.int32),
        pltpu.VMEM((1, ROWS, HPD * 192), BF16),
        pltpu.VMEM((1, ROWS, HPD * DV), BF16),
        pltpu.VMEM((1, ROWS, HPD * DV), BF16),
        pltpu.VMEM((DL, 512), BF16),
        pltpu.VMEM((DL, 512), BF16),
        pltpu.VMEM((NY, 4, QR, 128), BF16),
        pltpu.VMEM((HPD, ROWS, 192), BF16),
        pltpu.VMEM((HPD, ROWS, DV), BF16),
        pltpu.VMEM((8, ROWS), F32),
        pltpu.VMEM((HPD, ROWS, 192), F32),
        pltpu.VMEM((NY, ROWS, 1024), BF16),
        pltpu.VMEM((NX, NY, GR, 128), BF16),
        pltpu.VMEM((4, NY, GR, 128), BF16),
        pltpu.VMEM((4, NY, GR, 128), BF16),
        pltpu.VMEM((NY, GR, 128), BF16),
        pltpu.VMEM((NY, GR, 128), BF16),
        pltpu.VMEM((GR, 128), BF16),
        pltpu.VMEM((GR, 128), BF16),
        pltpu.VMEM((NX, GR, 128), BF16),
        pltpu.VMEM((2, NZ, NY, 8, 1024), BF16),
        pltpu.VMEM((NZ, NY, 8, 1024), BF16),
        pltpu.VMEM((NY, NZ, 8, 512), BF16),
        pltpu.VMEM((NZ, NY, 8, 512), BF16),
        pltpu.VMEM((NY, NZ, 8, 512), BF16),
        pltpu.VMEM((NZ, NY, 8, 512), BF16),
        pltpu.VMEM((NZ, 8, 512), BF16),
        pltpu.VMEM((NY, 8, 512), BF16),
        pltpu.VMEM((NZ, 8, 512), BF16),
        pltpu.VMEM((NY, 8, 512), BF16),
        dma((9,)),
        dma((2,)), dma((2, 4, 2)), dma((2,)), dma((NY, 2)),
        dma((5,)), dma((5, 4)), dma((5,)), dma((5, 4)),
        dma((2,)), dma((2,)), dma((2,)),
        dma((2,)), dma((2,)), dma((2,)), dma((2,)), dma((2,)),
    ]
    dq, ax, guk, guv = pl.pallas_call(
        kernel,
        out_shape=(
            jax.ShapeDtypeStruct((1, ROWS, HPD * 192), BF16),
            jax.ShapeDtypeStruct((NX, GR, 128), BF16),
            jax.ShapeDtypeStruct((8, 512), BF16),
            jax.ShapeDtypeStruct((8, 512), BF16),
        ),
        in_specs=[hbm] * 9,
        out_specs=(vmem,) * 4,
        scratch_shapes=shapes,
        compiler_params=pltpu.CompilerParams(
            collective_id=0, has_side_effects=True, vmem_limit_bytes=VMEM_LIMIT
        ),
    )(
        *(
            pltpu.with_memory_space_constraint(a, pltpu.HBM)
            for a in (
                latent, jnp.transpose(rope, (0, 2, 1)), lse, positions,
                query, grad_out, attn_out, w_uk, w_uv,
            )
        )
    )
    dq, gl, gr, guk, guv = pl.pallas_call(
        finish,
        out_shape=(
            jax.ShapeDtypeStruct((1, ROWS, HPD * 192), BF16),
            jax.ShapeDtypeStruct((1, ROWS, DL), F32),
            jax.ShapeDtypeStruct((1, DR, ROWS), F32),
            jax.ShapeDtypeStruct((8, 512), BF16),
            jax.ShapeDtypeStruct((8, 512), BF16),
        ),
        in_specs=[vmem] * 4,
        out_specs=(vmem,) * 5,
        compiler_params=pltpu.CompilerParams(vmem_limit_bytes=8 * 1024 * 1024),
    )(dq, ax, guk, guv)
    return dq, gl, jnp.transpose(gr, (0, 2, 1)), guk, guv


def solution(mesh):
    return jax.shard_map(
        on_device,
        mesh=mesh,
        in_specs=(
            P("dp", "ctx", None),
            P("dp", "ctx", None),
            P("dp", "ctx", "head"),
            P("dp", "ctx", "head"),
            P("dp", "ctx", "head"),
            P("dp", "head", "ctx"),
            P("dp", None),
            P(None, "head"),
            P(None, "head"),
        ),
        out_specs=(
            P("dp", "ctx", "head"),
            P("dp", "ctx", None),
            P("dp", "ctx", None),
            P(("dp", "ctx"), "head"),
            P(("dp", "ctx"), "head"),
        ),
        check_vma=False,
    )
```

time: 80.8 us -> 71.4 us (0.88)
  local copies, waits for them, and re-layouts: 6.64 us -> 0 us
  Pallas kernels: 73.1 us -> 70.5 us
    unnamed x11 -> x0, local copies, waits for them, and re-layouts: 5.06 us -> none
    pallas_call x1, Pallas kernels: 73.1 us -> 69.7 us  [on_device(): pl.pallas_call(kernel, out_shape=(jax.ShapeDtypeStruct((1, ROWS, HPD * 19...]
    pallas_call x1 -> x0, local copies, waits for them, and re-layouts: 1.58 us -> none  [on_device(): pl.pallas_call(kernel, out_shape=(jax.ShapeDtypeStruct((1, ROWS, HPD * 19...]
where the time goes in v2:
time: 71.4 us; the launch traced here: 71.2 us
  Pallas kernels  70.5 us (99%)
    pallas_call x1, Pallas kernels, on_device(): pl.pallas_call(kernel, out_shape=(jax.ShapeDtypeStruct((1, ROWS, HPD * 19...  69.7 us

profile of v2, /device:TPU:2, one launch (start us, length us, event | category | flops | bytes accessed | tf_op | source)
XLA Modules:
  0.0 71.2 jit_solution(9257238357650187466)
XLA Ops:
  0.6 69.7 %shard_map.128 = (bf16[1,128,768]{2,1,0:T(8,128)(2,1)S(1)}, bf16[8,72,128]{2,1,0:T(8,128)(2,1)S(1)}, bf16[8,512]{1,0:T(8,128)(2,1)S(1)}, bf16[8,512]{1,0:T(8,128)(2,1)S(1)}) custom-call(bf16[1,128,512]{2,1,0:T(8,128)(2,1)} %lat_hbm.1, bf16[1,64,128]{2,1,0:T(8,128)(2,1)} %bitcast.2, f32[1,4,128]{2,1,0:T(4,128)} %lse_hbm.1, s32[1,1024]{1,0:T(1,128)} %pos_hbm.1, ...), custom_call_target="tpu_custom_call" | custom-call | tf_op jit(solution)/shard_map/pallas_call | solution.py:418
  70.4 0.8 %shard_map.129 = (bf16[1,128,768]{2,1,0:T(8,128)(2,1)}, f32[1,128,512]{2,1,0:T(8,128)}, f32[1,64,128]{2,1,0:T(8,128)}, bf16[8,512]{1,0:T(8,128)(2,1)}, bf16[8,512]{1,0:T(8,128)(2,1)}) custom-call(bf16[1,128,768]{2,1,0:T(8,128)(2,1)S(1)} %get-tuple-element.14.dq_ref, bf16[8,72,128]{2,1,0:T(8,128)(2,1)S(1)} %get-tuple-element.15.ax_ref, ...), custom_call_target="tpu_custom_call" | custom-call | tf_op jit(solution)/shard_map/pallas_call | solution.py:441

commit v3 on v2

--- a/solution.py
+++ b/solution.py
@@ -42,17 +42,17 @@
     lat_hbm, rope_hbm, lse_hbm, pos_hbm, q_hbm, go_hbm, ao_hbm, wuk_hbm, wuv_hbm,
     dq_out, ax_out, guk_out, guv_out,
     lat_ref, rope_ref, lse_ref, pos_ref, q_ref, go_ref, ao_ref, wuk_ref, wuv_ref,
-    kv_all, qh, gh, delta, dq_acc, dkv_all, glb, xl, xr, ysend, yrecv, zs, zr, axr,
+    kv_all, qh, gh, delta, dq_acc, dkv_all, glb, xb, ysend, yrecv, zs, zr, axr,
     wgb, wgc, wa, wb, wa_in, wb_in, wa2, wb2, wa2_in, wb2_in,
-    in_sem, ag_s, ag_r, agx_s, agx_r, xl_s, xl_r, xr_s, xr_r, y_sem, z_sem, ax_sem,
-    c_sem, wy_sem, wz_sem, wy2_sem, wz2_sem,
+    in_sem, ag_s, ag_r, x_s, x_r, y_sem, z_sem, ax_sem,
+    c_sem, wy_sem, wz_sem, wy2_sem, wz2_sem, up_sem, down_sem,
 ):
     dp = lax.axis_index("dp")
     y = lax.axis_index("ctx")
     head = lax.axis_index("head")
     c, zl = lax.rem(dp, 2), dp // 2
     x, zh = head // 2, lax.rem(head, 2)
-    side = lax.rem(x, 2)
+    z = zh * NZ + zl
 
     def to_y(v):
         return {"ctx": wrap(v, NY)}
@@ -66,11 +66,43 @@
     other_core = {"dp": zl * 2 + (1 - c)}
     other_half = {"head": x * 2 + (1 - zh)}
 
+    def on_line(v):
+        return {"dp": lax.rem(v, NZ) * 2 + c, "head": x * 2 + v // NZ}
+
+    def tell(sem, peer):
+        pl.semaphore_signal(sem, inc=1, device_id=peer, device_id_type=MESH)
+
     barrier = pltpu.get_barrier_semaphore()
-    peers = [to_y(y + 1), to_y(y - 1), to_x(x + 1), to_x(x - 1)]
-    peers += [to_z(zl + d) for d in range(1, NZ)] + [other_core, other_half]
+    peers = [to_y(y + 1), to_y(y - 1), to_x(x + 1), to_x(x - 1), to_x(x + 2), to_x(x - 2)]
+    peers.append(other_core)
     for peer in peers:
-        pl.semaphore_signal(barrier, inc=1, device_id=peer, device_id_type=MESH)
+        tell(barrier, peer)
+
+    @pl.when(z > 0)
+    def _():
+        tell(barrier, on_line(z - 1))
+
+    @pl.when(z < 7)
+    def _():
+        tell(barrier, on_line(z + 1))
+
+    def pass_word(j):
+        @pl.when((z >= 1) & (z + j <= 7))
+        def _():
+            tell(up_sem.at[j - 1], on_line(z - 1))
+
+        @pl.when((z <= 6) & (z - j >= 0))
+        def _():
+            tell(down_sem.at[j - 1], on_line(z + 1))
+
+    def take_word(j):
+        @pl.when(z + j <= 6)
+        def _():
+            pl.semaphore_wait(up_sem.at[j - 1], 1)
+
+        @pl.when(z - j >= 1)
+        def _():
+            pl.semaphore_wait(down_sem.at[j - 1], 1)
 
     loads = []
     for i, (a, b) in enumerate(
@@ -103,32 +135,23 @@
             ]
         kv_all[y, t, 128:144, :] = rope_ref[0, 16 * t : 16 * t + 16, :]
 
-    pl.semaphore_wait(barrier, len(peers))
-
-    ag, agx = {}, {}
-
-    def ag_step(k):
-        for part in range(2):
+    pl.semaphore_wait(barrier, len(peers) + jnp.minimum(z, 1) + jnp.minimum(7 - z, 1))
+
+    ag = {}
+
+    def ag_step(k, pieces=range(4)):
+        for part in pieces:
             for way, sign in ((0, 1), (1, -1)):
-                if k == 4 and part != way:
+                last = part // 2 == way
+                if k == 4 and not last:
                     continue
                 if k > 0:
                     ag[way, k - 1, part].wait_recv()
-                ref = kv_all.at[wrap(y - sign * k, NY), 2 * side + part]
-                if k < 3 or (k == 3 and part == way):
+                if k < 3 or (k == 3 and last):
+                    ref = kv_all.at[wrap(y - sign * k, NY), part]
                     ag[way, k, part] = send(
                         ref, ref, ag_s.at[way], ag_r.at[way, k, part], to_y(y + sign)
                     )
-                if k > 0:
-                    r = 2 * k - 1 + way if k < 4 else 7
-                    agx[r, part] = send(
-                        ref, ref, agx_s.at[part], agx_r.at[r, part], to_x(x + 1 - 2 * part)
-                    )
-
-    def agx_wait(group):
-        for r in range(*GROUPS[group]):
-            for part in range(2):
-                agx[r, part].wait_recv()
 
     def prepare():
         for load in loads[2:]:
@@ -150,7 +173,7 @@
     def rope_of(b):
         return jnp.concatenate([kv_all[b, t, 128:144, :] for t in range(4)], axis=0).T
 
-    def compute(group):
+    def compute(group, between=None):
         pos_q = pos_ref[:, pl.ds(pl.multiple_of(y * ROWS, ROWS), ROWS)].astype(F32)
         lo, hi = GROUPS[group]
         blocks = [wrap(y + OFFS[r], NY) for r in range(lo, hi)]
@@ -189,6 +212,8 @@
             rope_grad = part if rope_grad is None else rope_grad + part
             dks.append(dk[:, 0:128].astype(BF16))
             dvs.append(dv.astype(BF16))
+            if between is not None and h == 1:
+                between()
         dkn = jnp.concatenate(dks, axis=1)
         dvn = jnp.concatenate(dvs, axis=1)
         for i, b in enumerate(blocks):
@@ -205,52 +230,56 @@
                     ]
                 glb[s, lo + i, 64:72, :] = turned[8 * s : 8 * s + 8].astype(BF16)
 
-    arms = {}
-
-    def hops(group, way):
-        return 4 if (group + way) % 2 == 0 else 3
-
-    def chain(group, k):
+    sums = {}
+
+    def x_send(group, slot, src, step):
         lo, hi = GROUPS[group]
-        for way, sign, slots, s_sem, r_sem in (
-            (0, -1, xl, xl_s, xl_r),
-            (1, 1, xr, xr_s, xr_r),
+        sums[group, slot] = send(
+            src, xb.at[slot, lo:hi], x_s.at[slot], x_r.at[group, slot], to_x(x + step)
+        )
+
+    def x_start(group):
+        lo, hi = GROUPS[group]
+        g = 1 - 2 * (group % 2)
+        for slot, dest, step in (
+            (0, -4 * g, -2 * g), (1, -3 * g, -g), (2, 3 * g, g), (3, -g, -g), (4, g, g),
         ):
-            length = hops(group, way)
-            if k >= length:
-                continue
-            dest = wrap(x + sign * (length - k), NX)
-            own = glb.at[dest, lo:hi]
-            src = own
-            if k > 0:
-                arms[group, way, k - 1].wait_recv()
-                src = slots.at[k - 1, lo:hi]
-                src[...] = (src[...].astype(F32) + own[...].astype(F32)).astype(BF16)
-            arms[group, way, k] = send(
-                src, slots.at[k, lo:hi], s_sem.at[group], r_sem.at[group, k], to_x(x + sign)
-            )
-
-    def chain_end(group):
+            x_send(group, slot, glb.at[wrap(x + dest, NX), lo:hi], step)
+
+    def x_middle(group):
         lo, hi = GROUPS[group]
-        last = (hops(group, 0) - 1, hops(group, 1) - 1)
-        for way in (0, 1):
-            arms[group, way, last[way]].wait_recv()
-        total = (
-            glb[x, lo:hi].astype(F32)
-            + xl[last[0], lo:hi].astype(F32)
-            + xr[last[1], lo:hi].astype(F32)
-        )
+        g = 1 - 2 * (group % 2)
+        sums[group, 0].wait_recv()
+        sums[group, 1].wait_recv()
+        xb[0, lo:hi] = (
+            xb[0, lo:hi].astype(F32)
+            + xb[1, lo:hi].astype(F32)
+            + glb[wrap(x - 2 * g, NX), lo:hi].astype(F32)
+        ).astype(BF16)
+        x_send(group, 5, xb.at[0, lo:hi], -2 * g)
+        sums[group, 2].wait_recv()
+        xb[2, lo:hi] = (
+            xb[2, lo:hi].astype(F32) + glb[wrap(x + 2 * g, NX), lo:hi].astype(F32)
+        ).astype(BF16)
+        x_send(group, 6, xb.at[2, lo:hi], 2 * g)
+
+    def x_end(group):
+        lo, hi = GROUPS[group]
+        total = glb[x, lo:hi].astype(F32)
+        for slot in (3, 4, 5, 6):
+            sums[group, slot].wait_recv()
+            total += xb[slot, lo:hi].astype(F32)
         ysend[lo:hi] = total.astype(BF16)
         for r in range(lo, hi):
             if r > 0:
                 send(ysend.at[r], yrecv.at[r], y_sem.at[0], y_sem.at[1], to_y(y + OFFS[r]))
 
-    def weight_rows(z):
-        lat = kv_all[:, :, 32 * z : 32 * z + 32, :].reshape(NY * ROWS, 128)
+    def weight_rows(i):
+        lat = kv_all[:, :, 32 * i : 32 * i + 32, :].reshape(NY * ROWS, 128)
         rows = dot(lat, dkv_all[...].reshape(NY * ROWS, 1024), 0, 0)
         for half in range(2):
-            wgb[half, z] = rows[64 * half : 64 * half + 64].reshape(NY, 8, 1024).astype(BF16)
-        send(wgb.at[1 - c, z], wgc.at[z], c_sem.at[0], c_sem.at[1], other_core)
+            wgb[half, i] = rows[64 * half : 64 * half + 64].reshape(NY, 8, 1024).astype(BF16)
+        send(wgb.at[1 - c, i], wgc.at[i], c_sem.at[0], c_sem.at[1], other_core)
 
     def spread(src, dst, sem, n, me, to):
         order = (4, 3, 5, 2, 6, 1, 7) if n == 8 else (2, 1, 3)
@@ -267,58 +296,50 @@
         return total.astype(BF16)
 
     ag_step(0)
+    pass_word(1)
     prepare()
     compute(0)
-    chain(0, 0)
+    x_start(0)
     ag_step(1)
-    ag_step(2)
-    chain(0, 1)
-    agx_wait(1)
-    compute(1)
-    chain(1, 0)
-    ag_step(3)
-    chain(0, 2)
-    agx_wait(2)
-    compute(2)
-    chain(2, 0)
+    compute(1, lambda: ag_step(2, (0,)))
+    x_start(1)
+    take_word(1)
+    pass_word(2)
+    ag_step(2, (1, 2, 3))
+    x_middle(0)
+    compute(2, lambda: ag_step(3, (0,)))
+    x_start(2)
+    ag_step(3, (1, 2, 3))
+    x_middle(1)
+    x_end(0)
+    compute(3)
+    x_start(3)
+    take_word(2)
+    pass_word(3)
     ag_step(4)
-    chain(1, 1)
-    chain(0, 3)
-    agx_wait(3)
-    compute(3)
-    chain(3, 0)
-    chain(2, 1)
-    chain(1, 2)
-    agx_wait(4)
     compute(4)
-    chain(4, 0)
-    chain(3, 1)
-    chain(2, 2)
-    chain(1, 3)
-    chain_end(0)
+    x_start(4)
+    x_middle(2)
+    x_end(1)
     weight_rows(0)
     weight_rows(1)
-    chain(4, 1)
-    chain(3, 2)
-    chain(2, 3)
-    chain_end(1)
+    x_middle(3)
+    x_end(2)
     weight_rows(2)
     weight_rows(3)
-    chain(4, 2)
-    chain(3, 3)
-    chain_end(2)
+    x_middle(4)
     for h in range(HPD):
         dq_out[0, :, 192 * h : 192 * h + 192] = dq_acc[h].astype(BF16)
-    chain(4, 3)
-    chain_end(3)
-    chain_end(4)
+    take_word(3)
+    x_end(3)
 
     whole(wgc, c_sem).wait_recv()
-    for z in range(NZ):
-        both = (wgb[c, z].astype(F32) + wgc[z].astype(F32)).astype(BF16)
-        wa[:, z] = both[:, :, 0:512]
-        wb[z] = both[:, :, 512:1024]
+    for i in range(NZ):
+        both = (wgb[c, i].astype(F32) + wgc[i].astype(F32)).astype(BF16)
+        wa[:, i] = both[:, :, 0:512]
+        wb[i] = both[:, :, 512:1024]
     spread(wb, wb_in, wz_sem, NZ, zl, to_z)
+    x_end(4)
     spread(wa, wa_in, wy_sem, NY, y, to_y)
 
     whole(yrecv.at[1:8], y_sem).wait_recv()
@@ -345,12 +366,12 @@
     whole(axr.at[1:8], ax_sem).wait_recv()
     ax_out[...] = axr[...]
 
-    for sem in (ag_s.at[0], ag_s.at[1], agx_s.at[0], agx_s.at[1]):
-        copy_of(glb.at[1:8, 0:2], glb.at[1:8, 0:2], sem, sem, other_half).wait_send()
-    for way, slots, s_sem in ((0, xl, xl_s), (1, xr, xr_s)):
-        for group, (lo, hi) in enumerate(GROUPS):
-            part = slots.at[0 : hops(group, way), lo:hi]
-            copy_of(part, part, s_sem.at[group], s_sem.at[group], other_half).wait_send()
+    for way in (0, 1):
+        copy_of(
+            glb.at[1:8, 0:4], glb.at[1:8, 0:4], ag_s.at[way], ag_s.at[way], other_half
+        ).wait_send()
+    for slot in range(7):
+        copy_of(xb.at[slot], xb.at[slot], x_s.at[slot], x_s.at[slot], other_half).wait_send()
     for ref, sem in (
         (wgc, c_sem), (yrecv.at[1:8], y_sem), (zr, z_sem), (axr.at[1:8], ax_sem),
         (wb_in.at[1:4], wz_sem), (wa_in.at[1:8], wy_sem),
@@ -392,8 +413,7 @@
         pltpu.VMEM((HPD, ROWS, 192), F32),
         pltpu.VMEM((NY, ROWS, 1024), BF16),
         pltpu.VMEM((NX, NY, GR, 128), BF16),
-        pltpu.VMEM((4, NY, GR, 128), BF16),
-        pltpu.VMEM((4, NY, GR, 128), BF16),
+        pltpu.VMEM((7, NY, GR, 128), BF16),
         pltpu.VMEM((NY, GR, 128), BF16),
         pltpu.VMEM((NY, GR, 128), BF16),
         pltpu.VMEM((GR, 128), BF16),
@@ -410,10 +430,11 @@
         pltpu.VMEM((NZ, 8, 512), BF16),
         pltpu.VMEM((NY, 8, 512), BF16),
         dma((9,)),
-        dma((2,)), dma((2, 4, 2)), dma((2,)), dma((NY, 2)),
-        dma((5,)), dma((5, 4)), dma((5,)), dma((5, 4)),
+        dma((2,)), dma((2, 4, 4)),
+        dma((7,)), dma((5, 7)),
         dma((2,)), dma((2,)), dma((2,)),
         dma((2,)), dma((2,)), dma((2,)), dma((2,)), dma((2,)),
+        pltpu.SemaphoreType.REGULAR((3,)), pltpu.SemaphoreType.REGULAR((3,)),
     ]
     dq, ax, guk, guv = pl.pallas_call(
         kernel,

time: 71.4 us -> 66 us (0.924)
  Pallas kernels: 70.5 us -> 65.2 us
    pallas_call x1, Pallas kernels: 69.7 us -> 64.4 us  [on_device(): pl.pallas_call(kernel, out_shape=(jax.ShapeDtypeStruct((1, ROWS, HPD * 19...]
where the time goes in v3:
time: 66 us; the launch traced here: 65.8 us
  Pallas kernels  65.2 us (99%)
    pallas_call x1, Pallas kernels, on_device(): pl.pallas_call(kernel, out_shape=(jax.ShapeDtypeStruct((1, ROWS, HPD * 19...  64.4 us

profile of v3, /device:TPU:2, one launch (start us, length us, event | category | flops | bytes accessed | tf_op | source)
XLA Modules:
  0.0 65.8 jit_solution(15029812604914142727)
XLA Ops:
  0.6 64.4 %shard_map.128 = (bf16[1,128,768]{2,1,0:T(8,128)(2,1)S(1)}, bf16[8,72,128]{2,1,0:T(8,128)(2,1)S(1)}, bf16[8,512]{1,0:T(8,128)(2,1)S(1)}, bf16[8,512]{1,0:T(8,128)(2,1)S(1)}) custom-call(bf16[1,128,512]{2,1,0:T(8,128)(2,1)} %lat_hbm.1, bf16[1,64,128]{2,1,0:T(8,128)(2,1)} %bitcast.2, f32[1,4,128]{2,1,0:T(4,128)} %lse_hbm.1, s32[1,1024]{1,0:T(1,128)} %pos_hbm.1, ...), custom_call_target="tpu_custom_call" | custom-call | tf_op jit(solution)/shard_map/pallas_call | solution.py:439
  65.0 0.8 %shard_map.129 = (bf16[1,128,768]{2,1,0:T(8,128)(2,1)}, f32[1,128,512]{2,1,0:T(8,128)}, f32[1,64,128]{2,1,0:T(8,128)}, bf16[8,512]{1,0:T(8,128)(2,1)}, bf16[8,512]{1,0:T(8,128)(2,1)}) custom-call(bf16[1,128,768]{2,1,0:T(8,128)(2,1)S(1)} %get-tuple-element.14.dq_ref, bf16[8,72,128]{2,1,0:T(8,128)(2,1)S(1)} %get-tuple-element.15.ax_ref, ...), custom_call_target="tpu_custom_call" | custom-call | tf_op jit(solution)/shard_map/pallas_call | solution.py:462

commit v4 on v3

--- a/solution.py
+++ b/solution.py
@@ -78,28 +78,26 @@
     for peer in peers:
         tell(barrier, peer)
 
-    @pl.when(z > 0)
-    def _():
-        tell(barrier, on_line(z - 1))
-
     @pl.when(z < 7)
     def _():
         tell(barrier, on_line(z + 1))
 
-    def pass_word(j):
+    def pass_up(j):
         @pl.when((z >= 1) & (z + j <= 7))
         def _():
-            tell(up_sem.at[j - 1], on_line(z - 1))
-
+            tell(up_sem.at[j], on_line(z - 1))
+
+    def take_up(j):
+        @pl.when(z + j <= 6)
+        def _():
+            pl.semaphore_wait(up_sem.at[j], 1)
+
+    def pass_down(j):
         @pl.when((z <= 6) & (z - j >= 0))
         def _():
             tell(down_sem.at[j - 1], on_line(z + 1))
 
-    def take_word(j):
-        @pl.when(z + j <= 6)
-        def _():
-            pl.semaphore_wait(up_sem.at[j - 1], 1)
-
+    def take_down(j):
         @pl.when(z - j >= 1)
         def _():
             pl.semaphore_wait(down_sem.at[j - 1], 1)
@@ -135,7 +133,7 @@
             ]
         kv_all[y, t, 128:144, :] = rope_ref[0, 16 * t : 16 * t + 16, :]
 
-    pl.semaphore_wait(barrier, len(peers) + jnp.minimum(z, 1) + jnp.minimum(7 - z, 1))
+    pl.semaphore_wait(barrier, len(peers) + jnp.minimum(z, 1))
 
     ag = {}
 
@@ -296,41 +294,47 @@
         return total.astype(BF16)
 
     ag_step(0)
-    pass_word(1)
+    pass_up(0)
     prepare()
     compute(0)
     x_start(0)
     ag_step(1)
     compute(1, lambda: ag_step(2, (0,)))
     x_start(1)
-    take_word(1)
-    pass_word(2)
+    take_up(0)
+    pass_up(1)
+    pass_down(1)
     ag_step(2, (1, 2, 3))
     x_middle(0)
     compute(2, lambda: ag_step(3, (0,)))
     x_start(2)
+    take_up(1)
+    take_down(1)
+    pass_up(2)
+    pass_down(2)
     ag_step(3, (1, 2, 3))
-    x_middle(1)
+    compute(3, lambda: x_middle(1))
+    x_start(3)
+    take_up(2)
+    take_down(2)
+    pass_up(3)
+    pass_down(3)
+    ag_step(4)
+    compute(4, lambda: x_middle(2))
+    x_start(4)
     x_end(0)
-    compute(3)
-    x_start(3)
-    take_word(2)
-    pass_word(3)
-    ag_step(4)
-    compute(4)
-    x_start(4)
-    x_middle(2)
-    x_end(1)
     weight_rows(0)
     weight_rows(1)
-    x_middle(3)
-    x_end(2)
     weight_rows(2)
     weight_rows(3)
+    x_end(1)
+    x_middle(3)
     x_middle(4)
+    x_end(2)
     for h in range(HPD):
         dq_out[0, :, 192 * h : 192 * h + 192] = dq_acc[h].astype(BF16)
-    take_word(3)
+    take_up(3)
+    take_down(3)
     x_end(3)
 
     whole(wgc, c_sem).wait_recv()
@@ -350,14 +354,14 @@
     wb2[...] = summed(wb[zl], wb_in, NZ)
     spread(wb2, wb2_in, wy2_sem, NY, y, to_y)
 
+    whole(wa_in.at[1:8], wy_sem).wait_recv()
+    wa2[...] = summed(wa[y], wa_in, NY)
+    spread(wa2, wa2_in, wz2_sem, NZ, zl, to_z)
+
     z_copy.wait_recv()
     axr[x] = (zs[...].astype(F32) + zr[...].astype(F32)).astype(BF16)
     for d in (4, 3, 5, 2, 6, 1, 7):
         send(axr.at[x], axr.at[x], ax_sem.at[0], ax_sem.at[1], to_x(x + d))
-
-    whole(wa_in.at[1:8], wy_sem).wait_recv()
-    wa2[...] = summed(wa[y], wa_in, NY)
-    spread(wa2, wa2_in, wz2_sem, NZ, zl, to_z)
 
     whole(wb2_in.at[1:8], wy2_sem).wait_recv()
     guv_out[...] = summed(wb2[y], wb2_in, NY)
@@ -434,7 +438,7 @@
         dma((7,)), dma((5, 7)),
         dma((2,)), dma((2,)), dma((2,)),
         dma((2,)), dma((2,)), dma((2,)), dma((2,)), dma((2,)),
-        pltpu.SemaphoreType.REGULAR((3,)), pltpu.SemaphoreType.REGULAR((3,)),
+        pltpu.SemaphoreType.REGULAR((4,)), pltpu.SemaphoreType.REGULAR((3,)),
     ]
     dq, ax, guk, guv = pl.pallas_call(
         kernel,

time: 66 us -> 62.1 us (0.941)
  Pallas kernels: 65.2 us -> 61.3 us
    pallas_call x1, Pallas kernels: 64.4 us -> 60.4 us  [on_device(): pl.pallas_call(kernel, out_shape=(jax.ShapeDtypeStruct((1, ROWS, HPD * 19...]
where the time goes in v4:
time: 62.1 us; the launch traced here: 61.9 us
  Pallas kernels  61.3 us (99%)
  between operations  0.64 us (1%)
    pallas_call x1, Pallas kernels, on_device(): pl.pallas_call(kernel, out_shape=(jax.ShapeDtypeStruct((1, ROWS, HPD * 19...  60.4 us

profile of v4, /device:TPU:2, one launch (start us, length us, event | category | flops | bytes accessed | tf_op | source)
XLA Modules:
  0.0 61.9 jit_solution(12712058551992046904)
XLA Ops:
  0.6 60.4 %shard_map.128 = (bf16[1,128,768]{2,1,0:T(8,128)(2,1)S(1)}, bf16[8,72,128]{2,1,0:T(8,128)(2,1)S(1)}, bf16[8,512]{1,0:T(8,128)(2,1)S(1)}, bf16[8,512]{1,0:T(8,128)(2,1)S(1)}) custom-call(bf16[1,128,512]{2,1,0:T(8,128)(2,1)} %lat_hbm.1, bf16[1,64,128]{2,1,0:T(8,128)(2,1)} %bitcast.2, f32[1,4,128]{2,1,0:T(4,128)} %lse_hbm.1, s32[1,1024]{1,0:T(1,128)} %pos_hbm.1, ...), custom_call_target="tpu_custom_call" | custom-call | tf_op jit(solution)/shard_map/pallas_call | solution.py:443
  61.1 0.8 %shard_map.129 = (bf16[1,128,768]{2,1,0:T(8,128)(2,1)}, f32[1,128,512]{2,1,0:T(8,128)}, f32[1,64,128]{2,1,0:T(8,128)}, bf16[8,512]{1,0:T(8,128)(2,1)}, bf16[8,512]{1,0:T(8,128)(2,1)}) custom-call(bf16[1,128,768]{2,1,0:T(8,128)(2,1)S(1)} %get-tuple-element.14.dq_ref, bf16[8,72,128]{2,1,0:T(8,128)(2,1)S(1)} %get-tuple-element.15.ax_ref, ...), custom_call_target="tpu_custom_call" | custom-call | tf_op jit(solution)/shard_map/pallas_call | solution.py:466

commit v5 on v4

--- a/solution.py
+++ b/solution.py
@@ -279,9 +279,8 @@
             wgb[half, i] = rows[64 * half : 64 * half + 64].reshape(NY, 8, 1024).astype(BF16)
         send(wgb.at[1 - c, i], wgc.at[i], c_sem.at[0], c_sem.at[1], other_core)
 
-    def spread(src, dst, sem, n, me, to):
-        order = (4, 3, 5, 2, 6, 1, 7) if n == 8 else (2, 1, 3)
-        for d in order:
+    def spread(src, dst, sem, n, me, to, order=None):
+        for d in order or ((4, 3, 5, 2, 6, 1, 7) if n == 8 else (2, 1, 3)):
             send(src.at[wrap(me + d, n)], dst.at[d], sem.at[0], sem.at[1], to(me + d))
 
     def whole(ref, sem):
@@ -343,8 +342,9 @@
         wa[:, i] = both[:, :, 0:512]
         wb[i] = both[:, :, 512:1024]
     spread(wb, wb_in, wz_sem, NZ, zl, to_z)
+    spread(wa, wa_in, wy_sem, NY, y, to_y, (3, 2, 1))
     x_end(4)
-    spread(wa, wa_in, wy_sem, NY, y, to_y)
+    spread(wa, wa_in, wy_sem, NY, y, to_y, (4, 5, 6, 7))
 
     whole(yrecv.at[1:8], y_sem).wait_recv()
     zs[...] = summed(ysend[0], yrecv, NY)

time: 62.1 us -> 62.9 us (1.013)
  Pallas kernels: 61.3 us -> 62 us
    pallas_call x1, Pallas kernels: 60.4 us -> 61.2 us  [on_device(): pl.pallas_call(kernel, out_shape=(jax.ShapeDtypeStruct((1, ROWS, HPD * 19...]
where the time goes in v5:
time: 62.9 us; the launch traced here: 62.7 us
  Pallas kernels  62 us (99%)
  between operations  0.64 us (1%)
    pallas_call x1, Pallas kernels, on_device(): pl.pallas_call(kernel, out_shape=(jax.ShapeDtypeStruct((1, ROWS, HPD * 19...  61.2 us

profile of v5, /device:TPU:2, one launch (start us, length us, event | category | flops | bytes accessed | tf_op | source)
XLA Modules:
  0.0 62.7 jit_solution(11436874582643060462)
XLA Ops:
  0.6 61.2 %shard_map.128 = (bf16[1,128,768]{2,1,0:T(8,128)(2,1)S(1)}, bf16[8,72,128]{2,1,0:T(8,128)(2,1)S(1)}, bf16[8,512]{1,0:T(8,128)(2,1)S(1)}, bf16[8,512]{1,0:T(8,128)(2,1)S(1)}) custom-call(bf16[1,128,512]{2,1,0:T(8,128)(2,1)} %lat_hbm.1, bf16[1,64,128]{2,1,0:T(8,128)(2,1)} %bitcast.2, f32[1,4,128]{2,1,0:T(4,128)} %lse_hbm.1, s32[1,1024]{1,0:T(1,128)} %pos_hbm.1, ...), custom_call_target="tpu_custom_call" | custom-call | tf_op jit(solution)/shard_map/pallas_call | solution.py:443
  61.9 0.8 %shard_map.129 = (bf16[1,128,768]{2,1,0:T(8,128)(2,1)}, f32[1,128,512]{2,1,0:T(8,128)}, f32[1,64,128]{2,1,0:T(8,128)}, bf16[8,512]{1,0:T(8,128)(2,1)}, bf16[8,512]{1,0:T(8,128)(2,1)}) custom-call(bf16[1,128,768]{2,1,0:T(8,128)(2,1)S(1)} %get-tuple-element.14.dq_ref, bf16[8,72,128]{2,1,0:T(8,128)(2,1)S(1)} %get-tuple-element.15.ax_ref, ...), custom_call_target="tpu_custom_call" | custom-call | tf_op jit(solution)/shard_map/pallas_call | solution.py:466
